TPU v7x, 32 devices: a whole 2x2x4 slice. The times are simulated.
32 devices in a mesh: lat: 8 (over y, x, core), lon: 4 (over z).
Axes of the slice: x: 2, y: 2, z: 4, core: 2. Of those that a mesh axis runs over, the one named last changes fastest.
Arguments:
- current: bfloat16 [69, 256, 512], P(None, 'lat', 'lon')
- next_fields: bfloat16 [96, 256, 512], P(('lat', 'lon')), may hold values from -6 to 6
- reader_slot: int32 [69], replicated, may hold values from 0 to 95, as said below
- first_weight: bfloat16 [9, 256, 69], replicated, may hold values from -0.25 to 0.25
- first_bias: float32 [256], replicated, may hold values from -3 to 3
- second_weight: bfloat16 [9, 256, 256], replicated, may hold values from -0.125 to 0.125
- second_bias: float32 [256], replicated, may hold values from -3 to 3
Outputs:
- features: bfloat16 [256, 256, 512], P(None, 'lat', 'lon')
- next_tile: bfloat16 [69, 256, 512], P(None, 'lat', 'lon')
Inputs may be any that keep to these rules, and one draw needn't show every extreme that they name: `reader_slot`: the 69 entries are different slots.
All inputs are finite; a program needn't handle non-finite values.
Results may differ from a plain program's by a relative error of at most 0.0053.
Values may be sent and summed in bfloat16 or wider, within the bound.
A program may use at most 128 MiB of HBM per device.

v0:
```python
import jax
import jax.numpy as jnp
from jax import lax
from jax.sharding import PartitionSpec as P


def padded_2(block, sides, width, periodic):
    for axis, dim in sides:
        count = lax.axis_size(axis)
        forward = [(i, i + 1) for i in range(count - 1)]
        if periodic:
            forward.append((count - 1, 0))
        backward = [(target, source) for source, target in forward]
        low = lax.ppermute(
            lax.slice_in_dim(block, block.shape[dim] - width, None, axis=dim), axis, forward
        )
        high = lax.ppermute(lax.slice_in_dim(block, 0, width, axis=dim), axis, backward)
        block = jnp.concatenate([low, block, high], axis=dim)
    return block


def conv_valid(padded, weight, bias):
    rows = padded.shape[1] - 2
    cols = padded.shape[2] - 2
    total = jnp.zeros((weight.shape[1], rows, cols), jnp.float32)
    for tap in range(9):
        shifted = padded[:, tap // 3 : tap // 3 + rows, tap % 3 : tap % 3 + cols]
        total = total + jnp.einsum(
            "ok,khw->ohw", weight[tap], shifted, preferred_element_type=jnp.float32
        )
    return total + bias[:, None, None]


def regrid(next_fields, reader_slot):
    slot_dev, rows_all, cols_all = next_fields.shape
    n_lat = lax.axis_size("lat")
    n_lon = lax.axis_size("lon")
    lat_rows = rows_all // n_lat
    lon_cols = cols_all // n_lon
    blocks = next_fields.reshape(slot_dev, n_lat, lat_rows, n_lon, lon_cols)
    ordered = blocks.transpose(1, 3, 0, 2, 4).reshape(n_lat * n_lon, slot_dev, lat_rows, lon_cols)
    moved = lax.all_to_all(ordered, ("lat", "lon"), split_axis=0, concat_axis=1, tiled=True)
    moved = moved.reshape(n_lat * n_lon * slot_dev, lat_rows, lon_cols)
    return jnp.take(moved, reader_slot, axis=0)


def encode(current, first_weight, first_bias, second_weight, second_bias):
    values = current.astype(jnp.float32)
    lat_rows = values.shape[1]
    lon_cols = values.shape[2]
    cells = lat_rows * lax.axis_size("lat") * lon_cols * lax.axis_size("lon")
    total, squares = lax.psum(
        (jnp.sum(values, axis=(1, 2)), jnp.sum(values * values, axis=(1, 2))), ("lat", "lon")
    )
    mean = total / cells
    scale = 1.0 / jnp.sqrt(squares / cells - mean * mean + 1e-05)
    normed = ((values - mean[:, None, None]) * scale[:, None, None]).astype(jnp.bfloat16)
    tall = padded_2(normed, (("lat", 1),), 2, False)
    padded = padded_2(tall, (("lon", 2),), 2, True)
    hidden = jax.nn.gelu(conv_valid(padded, first_weight, first_bias), approximate=True)
    global_row = lax.axis_index("lat") * lat_rows + jnp.arange(lat_rows + 2, dtype=jnp.int32) - 1
    inside = (global_row >= 0) & (global_row < lat_rows * lax.axis_size("lat"))
    hidden = jnp.where(inside[None, :, None], hidden, 0.0).astype(jnp.bfloat16)
    return conv_valid(hidden, second_weight, second_bias).astype(jnp.bfloat16)


def body(current, next_fields, reader_slot, first_weight, first_bias, second_weight, second_bias):
    features = encode(current, first_weight, first_bias, second_weight, second_bias)
    next_tile = regrid(next_fields, reader_slot)
    return (features, next_tile)


def solution(mesh):
    in_specs = (P(None, "lat", "lon"), P(("lat", "lon"), None, None), P(), P(), P(), P(), P())
    out_specs = (P(None, "lat", "lon"), P(None, "lat", "lon"))
    return jax.shard_map(body, mesh=mesh, in_specs=in_specs, out_specs=out_specs, check_vma=False)
```

profile of v0, /device:TPU:0, one launch (start us, length us, event | category | flops | bytes accessed | tf_op | source)
XLA Modules:
  0.0 146.5 jit_solution(17535352118714095713)
XLA Ops:
  0.6 1.8 %copy.13 = bf16[69,32,128]{0,2,1:T(8,128)(2,1)S(1)} copy(bf16[69,32,128]{2,1,0:T(8,128)(2,1)} %param.7) | data formatting | bytes 1130496 | tf_op args[0]
  3.1 42.0 %all-reduce = (f32[69]{0:T(128)S(1)}, f32[69]{0:T(128)S(1)}) all-reduce(f32[69]{0:T(128)S(1)} %get-tuple-element.9, f32[69]{0:T(128)S(1)} %get-tuple-element.8), channel_id=1, replica_groups=mesh['lat'=8,'lon'=4] {'lat','lon'}, use_global_device_ids=true, to_apply=%region_3.0 | all-reduce | flops 138 | bytes 1104 | tf_op jit(solution)/shard_map/psum | solution.py:52
  49.3 8.4 %all-to-all-start = ((bf16[32,3,32,128]{3,2,1,0:T(8,128)(2,1)}), bf16[32,3,32,128]{3,2,1,0:T(8,128)(2,1)}, u32[]{:S(2)}, u32[]{:S(2)}) async-start(bf16[32,3,32,128]{3,2,1,0:T(8,128)(2,1)} %bitcast.39), calls=%async_computation | async-start | bytes 1572864 | tf_op jit(solution)/shard_map/all_to_all | solution.py:42
  57.8 3.6 %collective-permute-start.3 = (bf16[69,36,2]{0,2,1:T(2,128)(2,1)S(1)}, bf16[69,36,2]{0,2,1:T(2,128)(2,1)S(1)}, u32[]{:S(2)}, u32[]{:S(2)}) collective-permute-start(bf16[69,36,2]{0,2,1:T(2,128)(2,1)S(1)} %get-tuple-element.13), channel_id=1, source_target_pairs={{1,0},{2,1},{3,2},{0,3},{5,4},{6,5},{7,6},{4,7},{9,8},{10,9},{11,1... | collective-permute-start | bytes 29816 | tf_op jit(solution)/shard_map/ppermute | solution.py:17
  61.4 10.1 %collective-permute-done.3 = bf16[69,36,2]{0,2,1:T(2,128)(2,1)S(1)} collective-permute-done((bf16[69,36,2]{0,2,1:T(2,128)(2,1)S(1)}, bf16[69,36,2]{0,2,1:T(2,128)(2,1)S(1)}, u32[]{:S(2)}, u32[]{:S(2)}) %collective-permute-start.3) | collective-permute-done | bytes 9968 | tf_op jit(solution)/shard_map/ppermute | solution.py:17
  71.5 4.1 %collective-permute-done.2 = bf16[69,36,2]{0,2,1:T(2,128)(2,1)S(1)} collective-permute-done((bf16[69,36,2]{0,2,1:T(2,128)(2,1)S(1)}, bf16[69,36,2]{0,2,1:T(2,128)(2,1)S(1)}, u32[]{:S(2)}, u32[]{:S(2)}) %collective-permute-start.2) | collective-permute-done | bytes 9968 | tf_op jit(solution)/shard_map/ppermute | solution.py:14
  76.9 3.0 %fusion.34 = f32[34,130,256]{2,1,0:T(8,128)} fusion(bf16[69,36,132]{0,2,1:T(8,128)(2,1)S(1)} %pad_maximum_fusion, bf16[9,256,69]{1,2,0:T(8,128)(2,1)S(1)} %copy-done.2), kind=kOutput, calls=%fused_computation.41 | convolution fusion | flops 156149760 | bytes 5746688 | tf_op jit(solution)/shard_map/ok,khw->ohw/dot_general | solution.py:28
  79.9 2.9 %fusion.36 = f32[34,130,256]{2,1,0:T(8,128)} fusion(bf16[69,36,132]{0,2,1:T(8,128)(2,1)S(1)} %pad_maximum_fusion, bf16[9,256,69]{1,2,0:T(8,128)(2,1)S(1)} %copy-done.2), kind=kOutput, calls=%fused_computation.43 | convolution fusion | flops 156149760 | bytes 5746688 | tf_op jit(solution)/shard_map/ok,khw->ohw/dot_general | solution.py:28
  82.8 2.9 %fusion.63 = f32[34,130,256]{2,1,0:T(8,128)} fusion(bf16[9,256,69]{1,2,0:T(8,128)(2,1)S(1)} %copy-done.2, bf16[69,36,2]{0,2,1:T(2,128)(2,1)S(1)} %collective-permute-done.3, bf16[69,2,128]{0,2,1:T(8,128)(2,1)S(1)} %collective-permute-done.1, bf16[69,32,128]{0,2,1:T(8,128)(2,1)S(1)} %fusion.10, bf16[69,2,128]{0,2,1:T(8,128)(2,1)S(1)} %collective-permute-done), kind=kOutput, calls=%fused_computation.69 | convolution fusion | flops 158733120 | bytes 5761024 | tf_op jit(solution)/shard_map/ok,khw->ohw/dot_general | solution.py:28
  85.7 2.9 %fusion.66 = f32[34,130,256]{2,1,0:T(8,128)} fusion(bf16[9,256,69]{1,2,0:T(8,128)(2,1)S(1)} %copy-done.2, bf16[69,2,128]{0,2,1:T(8,128)(2,1)S(1)} %collective-permute-done.1, bf16[69,32,128]{0,2,1:T(8,128)(2,1)S(1)} %fusion.10, bf16[69,2,128]{0,2,1:T(8,128)(2,1)S(1)} %collective-permute-done, bf16[69,36,2]{0,2,1:T(2,128)(2,1)S(1)} %collective-permute-done.2), kind=kOutput, calls=%fused_computation.72 | convolution fusion | flops 158733120 | bytes 5761024 | tf_op jit(solution)/shard_map/ok,khw->ohw/dot_general | solution.py:28
  88.6 3.0 %fusion.68 = f32[34,130,256]{2,1,0:T(8,128)} fusion(bf16[9,256,69]{1,2,0:T(8,128)(2,1)S(1)} %copy-done.2, bf16[69,36,2]{0,2,1:T(2,128)(2,1)S(1)} %collective-permute-done.3, bf16[69,2,128]{0,2,1:T(8,128)(2,1)S(1)} %collective-permute-done.1, bf16[69,32,128]{0,2,1:T(8,128)(2,1)S(1)} %fusion.10, bf16[69,2,128]{0,2,1:T(8,128)(2,1)S(1)} %collective-permute-done), kind=kOutput, calls=%fused_computation.74 | convolution fusion | flops 158733120 | bytes 5761024 | tf_op jit(solution)/shard_map/ok,khw->ohw/dot_general | solution.py:28
  91.6 3.0 %fusion.71 = f32[34,130,256]{2,1,0:T(8,128)} fusion(bf16[9,256,69]{1,2,0:T(8,128)(2,1)S(1)} %copy-done.2, bf16[69,2,128]{0,2,1:T(8,128)(2,1)S(1)} %collective-permute-done.1, bf16[69,32,128]{0,2,1:T(8,128)(2,1)S(1)} %fusion.10, bf16[69,2,128]{0,2,1:T(8,128)(2,1)S(1)} %collective-permute-done, bf16[69,36,2]{0,2,1:T(2,128)(2,1)S(1)} %collective-permute-done.2), kind=kOutput, calls=%fused_computation.77 | convolution fusion | flops 158733120 | bytes 5761024 | tf_op jit(solution)/shard_map/ok,khw->ohw/dot_general | solution.py:28
  94.6 2.9 %fusion.61 = f32[34,130,256]{2,1,0:T(8,128)} fusion(bf16[9,256,69]{1,2,0:T(8,128)(2,1)S(1)} %copy-done.2, bf16[69,2,128]{0,2,1:T(8,128)(2,1)S(1)} %collective-permute-done.1, bf16[69,32,128]{0,2,1:T(8,128)(2,1)S(1)} %fusion.10, bf16[69,2,128]{0,2,1:T(8,128)(2,1)S(1)} %collective-permute-done, bf16[69,36,2]{0,2,1:T(2,128)(2,1)S(1)} %collective-permute-done.2), kind=kOutput, calls=%fused_computation.67 | convolution fusion | flops 158733120 | bytes 5761024 | tf_op jit(solution)/shard_map/ok,khw->ohw/dot_general | solution.py:28
  97.5 12.7 %fusion.8 = bf16[256,34,130]{0,2,1:T(8,128)(2,1)S(1)} fusion(f32[34,130,256]{2,1,0:T(8,128)S(1)} %fusion.32, f32[34,130,256]{2,1,0:T(8,128)} %fusion.61, f32[34,130,256]{2,1,0:T(8,128)} %fusion.63, f32[34,130,256]{2,1,0:T(8,128)} %fusion.34, f32[34,130,256]{2,1,0:T(8,128)} %fusion.66, f32[34,130,256]{2,1,0:T(8,128)} %fusion.68, ...), kind=kOutput, calls=%fused_computation.10 | convolution fusion | flops 180232000 | bytes 39917056 | tf_op jit(solution)/shard_map/ok,khw->ohw/dot_general | solution.py:28
  111.0 2.7 %fusion.15 = f32[32,128,256]{2,1,0:T(8,128)} fusion(bf16[256,34,130]{0,2,1:T(8,128)(2,1)S(1)} %fusion.8, bf16[9,256,256]{2,1,0:T(8,128)(2,1)S(1)} %copy-done), kind=kOutput, calls=%fused_computation.21 | convolution fusion | flops 536870912 | bytes 6422528 | tf_op jit(solution)/shard_map/ok,khw->ohw/dot_general | solution.py:28
  113.7 2.7 %fusion.17 = f32[32,128,256]{2,1,0:T(8,128)} fusion(bf16[256,34,130]{0,2,1:T(8,128)(2,1)S(1)} %fusion.8, bf16[9,256,256]{2,1,0:T(8,128)(2,1)S(1)} %copy-done), kind=kOutput, calls=%fused_computation.23 | convolution fusion | flops 536870912 | bytes 6422528 | tf_op jit(solution)/shard_map/ok,khw->ohw/dot_general | solution.py:28
  116.4 2.7 %fusion.19 = f32[32,128,256]{2,1,0:T(8,128)} fusion(bf16[256,34,130]{0,2,1:T(8,128)(2,1)S(1)} %fusion.8, bf16[9,256,256]{2,1,0:T(8,128)(2,1)S(1)} %copy-done), kind=kOutput, calls=%fused_computation.25 | convolution fusion | flops 536870912 | bytes 6422528 | tf_op jit(solution)/shard_map/ok,khw->ohw/dot_general | solution.py:28
  119.1 2.7 %fusion.21 = f32[32,128,256]{2,1,0:T(8,128)} fusion(bf16[256,34,130]{0,2,1:T(8,128)(2,1)S(1)} %fusion.8, bf16[9,256,256]{2,1,0:T(8,128)(2,1)S(1)} %copy-done), kind=kOutput, calls=%fused_computation.27 | convolution fusion | flops 536870912 | bytes 6422528 | tf_op jit(solution)/shard_map/ok,khw->ohw/dot_general | solution.py:28
  121.8 2.7 %fusion.23 = f32[32,128,256]{2,1,0:T(8,128)} fusion(bf16[256,34,130]{0,2,1:T(8,128)(2,1)S(1)} %fusion.8, bf16[9,256,256]{2,1,0:T(8,128)(2,1)S(1)} %copy-done), kind=kOutput, calls=%fused_computation.29 | convolution fusion | flops 536870912 | bytes 6422528 | tf_op jit(solution)/shard_map/ok,khw->ohw/dot_general | solution.py:28
  124.5 2.7 %fusion.25 = f32[32,128,256]{2,1,0:T(8,128)} fusion(bf16[256,34,130]{0,2,1:T(8,128)(2,1)S(1)} %fusion.8, bf16[9,256,256]{2,1,0:T(8,128)(2,1)S(1)} %copy-done), kind=kOutput, calls=%fused_computation.31 | convolution fusion | flops 536870912 | bytes 6422528 | tf_op jit(solution)/shard_map/ok,khw->ohw/dot_general | solution.py:28
  127.2 2.7 %fusion.27 = f32[32,128,256]{2,1,0:T(8,128)} fusion(bf16[256,34,130]{0,2,1:T(8,128)(2,1)S(1)} %fusion.8, bf16[9,256,256]{2,1,0:T(8,128)(2,1)S(1)} %copy-done), kind=kOutput, calls=%fused_computation.33 | convolution fusion | flops 536870912 | bytes 6422528 | tf_op jit(solution)/shard_map/ok,khw->ohw/dot_general | solution.py:28
  129.9 10.8 %fusion.29 = bf16[256,32,128]{0,2,1:T(8,128)(2,1)S(1)} fusion(f32[256]{0:T(256)S(1)} %copy-done.4, bf16[256,34,130]{0,2,1:T(8,128)(2,1)S(1)} %fusion.8, f32[32,128,256]{2,1,0:T(8,128)S(1)} %fusion.13, f32[32,128,256]{2,1,0:T(8,128)} %fusion.15, f32[32,128,256]{2,1,0:T(8,128)} %fusion.17, f32[32,128,256]{2,1,0:T(8,128)} %fusion.19, ...), kind=kOutput, calls=%fused_computation.35 | convolution fusion | flops 547356672 | bytes 37880832 | tf_op jit(solution)/shard_map/ok,khw->ohw/dot_general | solution.py:28
  140.7 3.1 %copy.15 = bf16[256,32,128]{2,1,0:T(8,128)(2,1)} copy(bf16[256,32,128]{0,2,1:T(8,128)(2,1)S(1)} %fusion.29) | data formatting | bytes 4194304
  143.8 1.8 %gather_fusion = bf16[69,32,128]{2,1,0:T(8,128)(2,1)S(1)} fusion(bf16[96,32,128]{2,1,0:T(8,128)(2,1)} %bitcast.40, s32[1024]{0:T(1024)S(1)} %pad_clamp_fusion), kind=kCustom, calls=%fused_computation | custom fusion | bytes 1130772 | tf_op jit(solution)/shard_map/jit(_take)/gather | solution.py:44
  (33 shorter events, 7.8 us)
Async XLA Ops:
  0.6 47.4 %copy-start.1 = (bf16[3,256,512]{2,1,0:T(8,128)(2,1)S(1)}, bf16[3,256,512]{2,1,0:T(8,128)(2,1)}, u32[]{:S(2)}) copy-start(bf16[3,256,512]{2,1,0:T(8,128)(2,1)} %param.8) | copy-start | bytes 2359300
  45.4 12.3 %copy-start.5 = (s32[69]{0:T(128)S(1)}, s32[69]{0:T(128)}, u32[]{:S(2)}) copy-start(s32[69]{0:T(128)} %param.9) | copy-start | bytes 832
  45.4 12.3 %collective-permute-start = (bf16[69,2,128]{0,2,1:T(8,128)(2,1)S(1)}, bf16[69,2,128]{0,2,1:T(8,128)(2,1)S(1)}, u32[]{:S(2)}, u32[]{:S(2)}) collective-permute-start(bf16[69,2,128]{0,2,1:T(8,128)(2,1)S(1)} %get-tuple-element.14), channel_id=1, source_target_pairs={{0,4},{4,8},{8,12},{12,16},{16,20},{20,24},{24,28},{1,5},{5,9},{9,... | collective-permute-start | bytes 105992 | tf_op jit(solution)/shard_map/ppermute | solution.py:14
  46.7 11.0 %collective-permute-start.1 = (bf16[69,2,128]{0,2,1:T(8,128)(2,1)S(1)}, bf16[69,2,128]{0,2,1:T(8,128)(2,1)S(1)}, u32[]{:S(2)}, u32[]{:S(2)}) collective-permute-start(bf16[69,2,128]{0,2,1:T(8,128)(2,1)S(1)} %get-tuple-element.15), channel_id=1, source_target_pairs={{4,0},{8,4},{12,8},{16,12},{20,16},{24,20},{28,24},{5,1},{9,5},{13... | collective-permute-start | bytes 105992 | tf_op jit(solution)/shard_map/ppermute | solution.py:17
  49.3 26.9 %copy-start.2 = (bf16[9,256,69]{1,2,0:T(8,128)(2,1)S(1)}, bf16[9,256,69]{1,2,0:T(8,128)(2,1)}, u32[]{:S(2)}) copy-start(bf16[9,256,69]{1,2,0:T(8,128)(2,1)} %param.10) | copy-start | bytes 953860
  49.3 94.5 %all-to-all-start = ((bf16[32,3,32,128]{3,2,1,0:T(8,128)(2,1)}), bf16[32,3,32,128]{3,2,1,0:T(8,128)(2,1)}, u32[]{:S(2)}, u32[]{:S(2)}) async-start(bf16[32,3,32,128]{3,2,1,0:T(8,128)(2,1)} %bitcast.39), calls=%async_computation | async-start | bytes 1572864 | tf_op jit(solution)/shard_map/all_to_all | solution.py:42
  57.8 13.7 %collective-permute-start.3 = (bf16[69,36,2]{0,2,1:T(2,128)(2,1)S(1)}, bf16[69,36,2]{0,2,1:T(2,128)(2,1)S(1)}, u32[]{:S(2)}, u32[]{:S(2)}) collective-permute-start(bf16[69,36,2]{0,2,1:T(2,128)(2,1)S(1)} %get-tuple-element.13), channel_id=1, source_target_pairs={{1,0},{2,1},{3,2},{0,3},{5,4},{6,5},{7,6},{4,7},{9,8},{10,9},{11,1... | collective-permute-start | bytes 29816 | tf_op jit(solution)/shard_map/ppermute | solution.py:17
  61.4 14.3 %collective-permute-start.2 = (bf16[69,36,2]{0,2,1:T(2,128)(2,1)S(1)}, bf16[69,36,2]{0,2,1:T(2,128)(2,1)S(1)}, u32[]{:S(2)}, u32[]{:S(2)}) collective-permute-start(bf16[69,36,2]{0,2,1:T(2,128)(2,1)S(1)} %get-tuple-element.12), channel_id=1, source_target_pairs={{0,1},{1,2},{2,3},{3,0},{4,5},{5,6},{6,7},{7,4},{8,9},{9,10},{10,1... | collective-permute-start | bytes 29816 | tf_op jit(solution)/shard_map/ppermute | solution.py:14
  94.6 2.9 %copy-start.3 = (f32[256]{0:T(256)S(1)}, f32[256]{0:T(256)}, u32[]{:S(2)}) copy-start(f32[256]{0:T(256)} %param.11) | copy-start | bytes 3076
  97.5 12.7 %copy-start = (bf16[9,256,256]{2,1,0:T(8,128)(2,1)S(1)}, bf16[9,256,256]{2,1,0:T(8,128)(2,1)}, u32[]{:S(2)}) copy-start(bf16[9,256,256]{2,1,0:T(8,128)(2,1)} %param.12) | copy-start | bytes 3538948
  127.2 2.7 %copy-start.4 = (f32[256]{0:T(256)S(1)}, f32[256]{0:T(256)}, u32[]{:S(2)}) copy-start(f32[256]{0:T(256)} %param.13) | copy-start | bytes 3076
where the time goes:
time: 148 us; the launch traced here: 147 us
  matrix products  64.5 us (44%)
  blocking collectives  42 us (28%)
  starting transfers between devices  14.6 us (10%)
  waiting for transfers between devices  14.3 us (10%)
  local copies, waits for them, and re-layouts  7.99 us (5%)
  other arithmetic  2.36 us (2%)
    dot_general x18, matrix products, conv_valid(): jnp.einsum('ok,khw->ohw', weight[tap], shifted, preferred_element_type=jn...  64.5 us
    psum x1, blocking collectives, encode(): lax.psum((jnp.sum(values, axis=(1, 2)), jnp.sum(values * values, axis=(1,...  42 us
    ppermute x2, waiting for transfers between devices, padded_2(): lax.ppermute(lax.slice_in_dim(block, 0, width, axis=dim), axis, backward)  10.1 us
    all_to_all x1, starting transfers between devices, regrid(): lax.all_to_all(ordered, ('lat', 'lon'), split_axis=0, concat_axis=1, tile...  8.39 us
    unnamed x14, local copies, waits for them, and re-layouts  4.93 us
    ppermute x2, starting transfers between devices, padded_2(): lax.ppermute(lax.slice_in_dim(block, 0, width, axis=dim), axis, backward)  4.9 us
    ppermute x2, waiting for transfers between devices, padded_2(): lax.ppermute(lax.slice_in_dim(block, block.shape[dim] - width, None, axis...  4.15 us
  transfers between devices with their start and end apart: 5, of which 2 were waited for; matrix products, arithmetic and copies ran while one was open for 47% of the time, Pallas kernels for 0%

commit v1 on v0

v1 whole, which is shorter than its diff:
```python
import functools

import jax
import jax.numpy as jnp
from jax import lax
from jax.experimental import pallas as pl
from jax.experimental.pallas import tpu as pltpu
from jax.sharding import PartitionSpec as P

MESH = pl.DeviceIdType.MESH
F32 = jnp.float32
BF16 = jnp.bfloat16
LANES = 128


def gelu(v):
    return 0.5 * v * (1.0 + jnp.tanh(0.7978845608028654 * (v + 0.044715 * v * v * v)))


def kernel(
    dims, cur, nf, slot, w1, b1, w2, b2, feat, tile,
    xf, xt, cols, hcol, en, eh, xs, hs, w1s, w2s, stats, moved,
    st_send, st_recv, ha_send, ha_recv, mv_send, mv_recv, own_sem,
):
    n_lat, n_lon, chans, rows, wide, slots, hid = dims
    n = n_lat * n_lon
    kp = LANES
    cp = -(-chans // 8) * 8
    lat = lax.axis_index("lat")
    lon = lax.axis_index("lon")
    me = lat * n_lon + lon

    barrier = pltpu.get_barrier_semaphore()

    def greet(d, carry):
        t = lax.rem(me + d, n)
        pl.semaphore_signal(
            barrier, inc=1, device_id=(t // n_lon, lax.rem(t, n_lon)), device_id_type=MESH
        )
        return carry

    lax.fori_loop(1, n, greet, 0)

    xf[pl.ds(0, chans * rows), :] = cur[...].astype(F32)
    if cp > chans:
        xf[pl.ds(chans * rows, (cp - chans) * rows), :] = jnp.zeros(((cp - chans) * rows, wide), F32)

    def turn(r, carry):
        total, square = carry
        a = xf[pl.ds(r, cp, stride=rows), :]
        a = jnp.concatenate([a, jnp.zeros((kp - cp, wide), F32)], axis=0)
        t = a.T
        xt[r + 2] = t.astype(BF16)
        cols[0, pl.ds(2 * r, 1), :] = t[0:1]
        cols[0, pl.ds(2 * r + 1, 1), :] = t[1:2]
        cols[1, pl.ds(2 * r, 1), :] = t[wide - 2 : wide - 1]
        cols[1, pl.ds(2 * r + 1, 1), :] = t[wide - 1 : wide]
        parts = t.reshape(wide // 8, 8, kp)
        return total + jnp.sum(parts, axis=0), square + jnp.sum(parts * parts, axis=0)

    zero = jnp.zeros((8, kp), F32)
    total, square = lax.fori_loop(0, rows, turn, (zero, zero))
    stats[pl.ds(me, 1), 0:1, :] = jnp.sum(total, axis=0, keepdims=True)[None]
    stats[pl.ds(me, 1), 1:2, :] = jnp.sum(square, axis=0, keepdims=True)[None]

    pl.semaphore_wait(barrier, n - 1)

    def stat_copy(d, source):
        t = lax.rem(me + d, n)
        return pltpu.make_async_remote_copy(
            src_ref=stats.at[source], dst_ref=stats.at[source],
            send_sem=st_send.at[d], recv_sem=st_recv.at[d],
            device_id=(t // n_lon, lax.rem(t, n_lon)), device_id_type=MESH,
        )

    def stat_start(d, carry):
        stat_copy(d, me).start()
        return carry

    lax.fori_loop(1, n, stat_start, 0)

    north, south = lax.rem(lat + n_lat - 1, n_lat), lax.rem(lat + 1, n_lat)
    west, east = lax.rem(lon + n_lon - 1, n_lon), lax.rem(lon + 1, n_lon)
    halos = []
    for side, col_to in ((0, west), (1, east)):
        into = 1 - side
        halos.append((cols.at[side], hcol.at[into, pl.ds(8, 2 * rows)], (lat, col_to)))
        halos.append((cols.at[side, pl.ds(0, 8)], hcol.at[into, pl.ds(8 + 2 * rows, 8)], (north, col_to)))
        halos.append((cols.at[side, pl.ds(2 * rows - 8, 8)], hcol.at[into, pl.ds(0, 8)], (south, col_to)))
    halos.append((xt.at[pl.ds(2, 2)], xt.at[pl.ds(rows + 2, 2)], (north, lon)))
    halos.append((xt.at[pl.ds(rows, 2)], xt.at[pl.ds(0, 2)], (south, lon)))
    copies = [
        pltpu.make_async_remote_copy(
            src_ref=src, dst_ref=dst, send_sem=ha_send.at[i], recv_sem=ha_recv.at[i],
            device_id=where, device_id_type=MESH,
        )
        for i, (src, dst, where) in enumerate(halos)
    ]
    for copy in copies:
        copy.start()

    def field_copy(d, source):
        t = lax.rem(me + d, n)
        tl, tn = t // n_lon, lax.rem(t, n_lon)
        return pltpu.make_async_remote_copy(
            src_ref=nf.at[:, pl.ds(pl.multiple_of(tl * rows, rows), rows), pl.ds(pl.multiple_of(tn * wide, wide), wide)],
            dst_ref=moved.at[pl.ds(source * slots, slots)],
            send_sem=mv_send.at[d], recv_sem=mv_recv.at[d],
            device_id=(tl, tn), device_id_type=MESH,
        )

    def field_start(d, carry):
        field_copy(d, me).start()
        return carry

    lax.fori_loop(1, n, field_start, 0)
    own = pltpu.make_async_copy(
        nf.at[:, pl.ds(pl.multiple_of(lat * rows, rows), rows), pl.ds(pl.multiple_of(lon * wide, wide), wide)],
        moved.at[pl.ds(me * slots, slots)],
        own_sem,
    )
    own.start()

    for tap in range(9):
        w1s[pl.ds(tap * kp, kp), :] = jnp.concatenate(
            [w1[tap].astype(F32), jnp.zeros((kp - chans, hid), F32)], axis=0
        ).astype(BF16)

    def turn_weight(tap, carry):
        w2s[pl.ds(pl.multiple_of(tap * hid, hid), hid), :] = w2[tap].astype(F32).T.astype(BF16)
        return carry

    lax.fori_loop(0, 9, turn_weight, 0)

    def stat_wait(d, carry):
        copy = stat_copy(d, lax.rem(me - d + n, n))
        copy.wait_recv()
        return carry

    lax.fori_loop(1, n, stat_wait, 0)
    sums = jnp.sum(stats[...], axis=0)
    cells = n * rows * wide
    mean = sums[0:1] / cells
    scale = 1.0 / jnp.sqrt(sums[1:2] / cells - mean * mean + 1e-05)

    for copy in copies:
        copy.wait_recv()

    first = jnp.where(lat == 0, 0, -2)
    last = jnp.where(lat == n_lat - 1, rows - 1, rows + 1)
    tall = rows + 4
    step = en.shape[1]

    line = lax.broadcasted_iota(jnp.int32, (step, 1), 0) - 2
    inside = (line >= first) & (line <= last)
    en[...] = jnp.zeros_like(en)
    for side in range(2):
        mid = 2 if side == 0 else 0
        for j in range(2):
            en[3 * side + (j if side == 0 else j + 1), pl.ds(0, tall), :] = hcol[side, pl.ds(4 + j, tall, stride=2), :]
        at = 0 if side == 0 else wide - 1
        base = 0 if side == 0 else wide - 16
        en[3 * side + mid, pl.ds(2, rows), :] = cols[side, pl.ds(0 if side == 0 else 1, rows, stride=2), :]
        for p in (0, 1, rows + 2, rows + 3):
            en[3 * side + mid, pl.ds(p, 1), :] = xt[p, pl.ds(base, 16), :].astype(F32)[at - base : at - base + 1]
    for k in range(6):
        en[k] = jnp.where(inside, (en[k] - mean) * scale, 0.0)
    bias1 = b1[...]
    bias2 = b2[...]
    hline = lax.broadcasted_iota(jnp.int32, (rows + 2, 1), 0) - 1
    hinside = (hline >= first) & (hline <= last)
    for side in range(2):
        edge = jnp.concatenate([en[3 * side + k] for k in range(3)], axis=1).astype(BF16)
        z = [
            jnp.dot(edge, w1s[pl.ds(3 * a * kp, 3 * kp), :], preferred_element_type=F32)
            for a in range(3)
        ]
        h = z[0][0 : rows + 2] + z[1][1 : rows + 3] + z[2][2 : rows + 4] + bias1
        eh[side, pl.ds(0, rows + 2), :] = jnp.where(hinside, gelu(h), 0.0)

    spot = lax.broadcasted_iota(jnp.int32, (wide, 1), 0)

    def spread(x, left, right):
        lo = jnp.where(spot == 0, left, pltpu.roll(x, 1, 0))
        hi = jnp.where(spot == wide - 1, right, pltpu.roll(x, wide - 1, 0))
        return lo.astype(BF16), x.astype(BF16), hi.astype(BF16)

    def normal(p, carry):
        ok = (p - 2 >= first) & (p - 2 <= last)
        x = (xt[p].astype(F32) - mean) * scale
        x = jnp.where(ok, x, 0.0)
        three = spread(x, en[1, pl.ds(p, 1), :], en[4, pl.ds(p, 1), :])
        for k in range(3):
            xs[p, :, k * kp : (k + 1) * kp] = three[k]
        return carry

    lax.fori_loop(0, tall, normal, 0)

    def one(b, carry):
        q = 2 * b
        left = jnp.concatenate(
            [xs[pl.ds(q + a, 2)].reshape(2 * wide, 3 * kp) for a in range(3)], axis=1
        )
        h = gelu(jnp.dot(left, w1s[...], preferred_element_type=F32) + bias1)
        for k in range(2):
            ok = (q + k - 1 >= first) & (q + k - 1 <= last)
            x = jnp.where(ok, h[k * wide : (k + 1) * wide], 0.0)
            three = spread(x, eh[0, pl.ds(q + k, 1), :], eh[1, pl.ds(q + k, 1), :])
            for m in range(3):
                hs[q + k, :, m * hid : (m + 1) * hid] = three[m]
        return carry

    lax.fori_loop(0, (rows + 2) // 2, one, 0)

    def two(b, carry):
        q = 2 * b
        left = jnp.concatenate(
            [hs[pl.ds(q + a, 2)].reshape(2 * wide, 3 * hid) for a in range(3)], axis=1
        )
        out = jnp.dot(left, w2s[...], preferred_element_type=F32) + bias2
        feat[pl.ds(pl.multiple_of(q * wide, 2 * wide), 2 * wide), :] = out.astype(BF16)
        return carry

    lax.fori_loop(0, rows // 2, two, 0)

    own.wait()

    def field_wait(d, carry):
        field_copy(d, lax.rem(me - d + n, n)).wait_recv()
        return carry

    lax.fori_loop(1, n, field_wait, 0)

    def take(c, carry):
        tile[c] = moved[slot[c]]
        return carry

    lax.fori_loop(0, chans, take, 0)

    def sent(d, carry):
        stat_copy(d, me).wait_send()
        field_copy(d, me).wait_send()
        return carry

    lax.fori_loop(1, n, sent, 0)
    for copy in copies:
        copy.wait_send()


def body(current, next_fields, reader_slot, first_weight, first_bias, second_weight, second_bias):
    n_lat, n_lon = lax.axis_size("lat"), lax.axis_size("lon")
    n = n_lat * n_lon
    chans, rows, wide = current.shape
    slots = next_fields.shape[0]
    hid = first_weight.shape[1]
    kp = LANES
    cp = -(-chans // 8) * 8
    step = -(-(rows + 4) // 16) * 16
    dims = (n_lat, n_lon, chans, rows, wide, slots, hid)
    vmem = pl.BlockSpec(memory_space=pltpu.VMEM)
    features, tile = pl.pallas_call(
        functools.partial(kernel, dims),
        out_shape=(
            jax.ShapeDtypeStruct((rows * wide, hid), BF16),
            jax.ShapeDtypeStruct((chans, rows, wide), BF16),
        ),
        in_specs=[
            vmem, pl.BlockSpec(memory_space=pl.ANY), pl.BlockSpec(memory_space=pltpu.SMEM),
            vmem, vmem, vmem, vmem,
        ],
        out_specs=(vmem, vmem),
        scratch_shapes=[
            pltpu.VMEM((cp * rows, wide), F32),
            pltpu.VMEM((rows + 4, wide, kp), BF16),
            pltpu.VMEM((2, 2 * rows, kp), F32),
            pltpu.VMEM((2, 2 * rows + 16, kp), F32),
            pltpu.VMEM((6, step, kp), F32),
            pltpu.VMEM((2, step, hid), F32),
            pltpu.VMEM((rows + 4, wide, 3 * kp), BF16),
            pltpu.VMEM((rows + 2, wide, 3 * hid), BF16),
            pltpu.VMEM((9 * kp, hid), BF16),
            pltpu.VMEM((9 * hid, hid), BF16),
            pltpu.VMEM((n, 2, kp), F32),
            pltpu.VMEM((n * slots, rows, wide), BF16),
            pltpu.SemaphoreType.DMA((n,)),
            pltpu.SemaphoreType.DMA((n,)),
            pltpu.SemaphoreType.DMA((8,)),
            pltpu.SemaphoreType.DMA((8,)),
            pltpu.SemaphoreType.DMA((n,)),
            pltpu.SemaphoreType.DMA((n,)),
            pltpu.SemaphoreType.DMA,
        ],
        compiler_params=pltpu.CompilerParams(
            collective_id=0, has_side_effects=True, vmem_limit_bytes=60 * 1024 * 1024
        ),
    )(
        current.reshape(chans * rows, wide), next_fields, reader_slot,
        first_weight.transpose(0, 2, 1), first_bias[None], second_weight, second_bias[None],
    )
    return features.reshape(rows, wide, hid).transpose(2, 0, 1), tile


def solution(mesh):
    in_specs = (P(None, "lat", "lon"), P(("lat", "lon"), None, None), P(), P(), P(), P(), P())
    out_specs = (P(None, "lat", "lon"), P(None, "lat", "lon"))
    return jax.shard_map(body, mesh=mesh, in_specs=in_specs, out_specs=out_specs, check_vma=False)
```

time: 148 us -> 42.4 us (0.29)
  matrix products: 64.5 us -> 0 us
  blocking collectives: 42 us -> 0 us
  Pallas kernels: 0 us -> 36.1 us
  starting transfers between devices: 14.6 us -> 0 us
  waiting for transfers between devices: 14.3 us -> 0 us
  local copies, waits for them, and re-layouts: 7.99 us -> 5.37 us
  other arithmetic: 2.36 us -> 0 us
    dot_general x18 -> x0, matrix products: 64.5 us -> none  [conv_valid(): jnp.einsum('ok,khw->ohw', weight[tap], shifted, preferred_element_type=jn...]
    psum x1 -> x0, blocking collectives: 42 us -> none  [encode(): lax.psum((jnp.sum(values, axis=(1, 2)), jnp.sum(values * values, axis=(1,...]
    pallas_call x0 -> x1, Pallas kernels: none -> 36.1 us  [body(): pl.pallas_call(functools.partial(kernel, dims), out_shape=(jax.ShapeDtype...]
    ppermute x4 -> x0, waiting for transfers between devices: 14.3 us -> none  [the longest x2 10.1 us: padded_2(): lax.ppermute(lax.slice_in_dim(block, 0, width, axis=dim), axis, backward)]
    all_to_all x1 -> x0, starting transfers between devices: 8.39 us -> none  [regrid(): lax.all_to_all(ordered, ('lat', 'lon'), split_axis=0, concat_axis=1, tile...]
    ppermute x4 -> x0, starting transfers between devices: 6.19 us -> none  [the longest x2 4.9 us: padded_2(): lax.ppermute(lax.slice_in_dim(block, 0, width, axis=dim), axis, backward)]
    reshape x1, local copies, waits for them, and re-layouts: 0.18 us -> 4.56 us  [body(): return (features.reshape(rows, wide, hid).transpose(2, 0, 1), tile)]
    unnamed x14 -> x3, local copies, waits for them, and re-layouts: 4.93 us -> 0.81 us
  transfers between devices with their start and end apart: 5 -> 0, of which waited for: 2 -> 0; matrix products, arithmetic and copies ran while one was open for 47% -> 0% of each run, Pallas kernels for 0% -> 0%
where the time goes in v1:
time: 42.4 us; the launch traced here: 42.1 us
  Pallas kernels  36.1 us (85%)
  local copies, waits for them, and re-layouts  5.37 us (13%)
  between operations  0.65 us (2%)
    pallas_call x1, Pallas kernels, body(): pl.pallas_call(functools.partial(kernel, dims), out_shape=(jax.ShapeDtype...  36.1 us
    reshape x1, local copies, waits for them, and re-layouts, body(): return (features.reshape(rows, wide, hid).transpose(2, 0, 1), tile)  4.56 us

profile of v1, /device:TPU:0, one launch (start us, length us, event | category | flops | bytes accessed | tf_op | source)
XLA Modules:
  0.0 42.1 jit_solution(7694758224026632265)
XLA Ops:
  0.6 36.1 %shard_map.86 = (bf16[4096,256]{1,0:T(8,128)(2,1)}, bf16[69,32,128]{2,1,0:T(8,128)(2,1)}) custom-call(bf16[2208,128]{1,0:T(8,128)(2,1)} %bitcast.8, bf16[3,256,512]{2,1,0:T(8,128)(2,1)} %nf.1, s32[69]{0:T(128)} %slot.1, bf16[9,69,256]{2,1,0:T(8,128)(2,1)} %bitcast.9, f32[1,256]{1,0:T(1,128)} %bitcast.10, bf16[9,256,256]{2,1,0:T(8,128)(2,1)} %w2.1, ...), custom_call_target="tpu_custom_call" | custom-call | tf_op jit(solution)/shard_map/pallas_call | solution.py:261
  36.8 0.0 copy-start
  36.8 4.6 %copy.9 = bf16[32,128,256]{1,0,2:T(8,128)(2,1)} copy(bf16[32,128,256]{2,1,0:T(8,128)(2,1)} %bitcast.7) | data formatting | bytes 4194304 | tf_op jit(solution)/shard_map/reshape | solution.py:300
  41.3 0.0 copy-done
  41.3 0.8 %copy.11 = bf16[69,32,128]{2,1,0:T(8,128)(2,1)} copy(bf16[69,32,128]{2,1,0:T(8,128)(2,1)S(1)} %copy-done) | data formatting | bytes 1130496
Async XLA Ops:
  36.8 4.6 %copy-start = (bf16[69,32,128]{2,1,0:T(8,128)(2,1)S(1)}, bf16[69,32,128]{2,1,0:T(8,128)(2,1)}, u32[]{:S(2)}) copy-start(bf16[69,32,128]{2,1,0:T(8,128)(2,1)} %get-tuple-element.9) | copy-start | bytes 1695748

commit v2 on v1

--- a/solution.py
+++ b/solution.py
@@ -11,6 +11,7 @@
 F32 = jnp.float32
 BF16 = jnp.bfloat16
 LANES = 128
+EARLY = 4
 
 
 def gelu(v):
@@ -18,17 +19,27 @@
 
 
 def kernel(
-    dims, cur, nf, slot, w1, b1, w2, b2, feat, tile,
-    xf, xt, cols, hcol, en, eh, xs, hs, w1s, w2s, stats, moved,
+    dims, cur_in, nf, slot_in, w1_in, b1_in, w2_in, b2_in, feat, tile,
+    cur, w1, w2, b1, b2, slot, yf, in_sem, xf, xt, cols, hcol, en, eh, xs, hs, w1s, w2s, stats, moved,
     st_send, st_recv, ha_send, ha_recv, mv_send, mv_recv, own_sem,
 ):
     n_lat, n_lon, chans, rows, wide, slots, hid = dims
     n = n_lat * n_lon
     kp = LANES
     cp = -(-chans // 8) * 8
+    pitch = xf.shape[1]
+    xflat = xf.reshape(cp * pitch, wide)
+    yflat = yf.reshape(hid * pitch, wide)
     lat = lax.axis_index("lat")
     lon = lax.axis_index("lon")
     me = lat * n_lon + lon
+
+    loads = [
+        pltpu.make_async_copy(src, dst, in_sem.at[i])
+        for i, (src, dst) in enumerate(((cur_in, cur), (w1_in, w1), (w2_in, w2), (b1_in, b1), (b2_in, b2), (slot_in, slot)))
+    ]
+    for load in loads:
+        load.start()
 
     barrier = pltpu.get_barrier_semaphore()
 
@@ -41,13 +52,39 @@
 
     lax.fori_loop(1, n, greet, 0)
 
-    xf[pl.ds(0, chans * rows), :] = cur[...].astype(F32)
+    loads[0].wait()
+    xf[0:chans, 0:rows, :] = cur[...].astype(F32)
     if cp > chans:
-        xf[pl.ds(chans * rows, (cp - chans) * rows), :] = jnp.zeros(((cp - chans) * rows, wide), F32)
+        xf[chans:cp, :, :] = jnp.zeros((cp - chans, pitch, wide), F32)
+
+    pl.semaphore_wait(barrier, n - 1)
+    early = min(EARLY, n)
+
+    def field_copy(d, source):
+        t = lax.rem(me + d, n)
+        tl, tn = t // n_lon, lax.rem(t, n_lon)
+        return pltpu.make_async_remote_copy(
+            src_ref=nf.at[:, pl.ds(pl.multiple_of(tl * rows, rows), rows), pl.ds(pl.multiple_of(tn * wide, wide), wide)],
+            dst_ref=moved.at[pl.ds(source * slots, slots)],
+            send_sem=mv_send.at[d], recv_sem=mv_recv.at[d],
+            device_id=(tl, tn), device_id_type=MESH,
+        )
+
+    def field_start(d, carry):
+        field_copy(d, me).start()
+        return carry
+
+    lax.fori_loop(1, early, field_start, 0)
+    own = pltpu.make_async_copy(
+        nf.at[:, pl.ds(pl.multiple_of(lat * rows, rows), rows), pl.ds(pl.multiple_of(lon * wide, wide), wide)],
+        moved.at[pl.ds(me * slots, slots)],
+        own_sem,
+    )
+    own.start()
 
     def turn(r, carry):
         total, square = carry
-        a = xf[pl.ds(r, cp, stride=rows), :]
+        a = xflat[pl.ds(r, cp, stride=pitch), :]
         a = jnp.concatenate([a, jnp.zeros((kp - cp, wide), F32)], axis=0)
         t = a.T
         xt[r + 2] = t.astype(BF16)
@@ -59,11 +96,9 @@
         return total + jnp.sum(parts, axis=0), square + jnp.sum(parts * parts, axis=0)
 
     zero = jnp.zeros((8, kp), F32)
-    total, square = lax.fori_loop(0, rows, turn, (zero, zero))
+    total, square = lax.fori_loop(0, rows, turn, (zero, zero), unroll=4)
     stats[pl.ds(me, 1), 0:1, :] = jnp.sum(total, axis=0, keepdims=True)[None]
     stats[pl.ds(me, 1), 1:2, :] = jnp.sum(square, axis=0, keepdims=True)[None]
-
-    pl.semaphore_wait(barrier, n - 1)
 
     def stat_copy(d, source):
         t = lax.rem(me + d, n)
@@ -99,28 +134,10 @@
     for copy in copies:
         copy.start()
 
-    def field_copy(d, source):
-        t = lax.rem(me + d, n)
-        tl, tn = t // n_lon, lax.rem(t, n_lon)
-        return pltpu.make_async_remote_copy(
-            src_ref=nf.at[:, pl.ds(pl.multiple_of(tl * rows, rows), rows), pl.ds(pl.multiple_of(tn * wide, wide), wide)],
-            dst_ref=moved.at[pl.ds(source * slots, slots)],
-            send_sem=mv_send.at[d], recv_sem=mv_recv.at[d],
-            device_id=(tl, tn), device_id_type=MESH,
-        )
-
-    def field_start(d, carry):
-        field_copy(d, me).start()
-        return carry
-
-    lax.fori_loop(1, n, field_start, 0)
-    own = pltpu.make_async_copy(
-        nf.at[:, pl.ds(pl.multiple_of(lat * rows, rows), rows), pl.ds(pl.multiple_of(lon * wide, wide), wide)],
-        moved.at[pl.ds(me * slots, slots)],
-        own_sem,
-    )
-    own.start()
-
+    lax.fori_loop(early, n, field_start, 0)
+
+    for load in loads[1:]:
+        load.wait()
     for tap in range(9):
         w1s[pl.ds(tap * kp, kp), :] = jnp.concatenate(
             [w1[tap].astype(F32), jnp.zeros((kp - chans, hid), F32)], axis=0
@@ -196,8 +213,15 @@
 
     lax.fori_loop(0, tall, normal, 0)
 
-    def one(b, carry):
-        q = 2 * b
+    def second(q):
+        left = jnp.concatenate(
+            [hs[pl.ds(q + a, 2)].reshape(2 * wide, 3 * hid) for a in range(3)], axis=1
+        )
+        out = jnp.dot(left, w2s[...], preferred_element_type=F32) + bias2
+        for k in range(2):
+            yflat[pl.ds(q + k, hid, stride=pitch), :] = out[k * wide : (k + 1) * wide].T
+
+    def first_conv(q):
         left = jnp.concatenate(
             [xs[pl.ds(q + a, 2)].reshape(2 * wide, 3 * kp) for a in range(3)], axis=1
         )
@@ -208,20 +232,21 @@
             three = spread(x, eh[0, pl.ds(q + k, 1), :], eh[1, pl.ds(q + k, 1), :])
             for m in range(3):
                 hs[q + k, :, m * hid : (m + 1) * hid] = three[m]
-        return carry
-
-    lax.fori_loop(0, (rows + 2) // 2, one, 0)
-
-    def two(b, carry):
-        q = 2 * b
-        left = jnp.concatenate(
-            [hs[pl.ds(q + a, 2)].reshape(2 * wide, 3 * hid) for a in range(3)], axis=1
-        )
-        out = jnp.dot(left, w2s[...], preferred_element_type=F32) + bias2
-        feat[pl.ds(pl.multiple_of(q * wide, 2 * wide), 2 * wide), :] = out.astype(BF16)
-        return carry
-
-    lax.fori_loop(0, rows // 2, two, 0)
+
+    def both(b, carry):
+        second(2 * b - 4)
+        first_conv(2 * b)
+        return carry
+
+    first_conv(0)
+    first_conv(2)
+    lax.fori_loop(2, (rows + 2) // 2, both, 0)
+    second(rows - 2)
+
+    chunk = hid // 8
+    for k in range(8):
+        part = pl.ds(k * chunk, chunk)
+        feat[part] = yf[part, 0:rows, :].astype(BF16)
 
     own.wait()
 
@@ -255,22 +280,31 @@
     hid = first_weight.shape[1]
     kp = LANES
     cp = -(-chans // 8) * 8
+    pitch = 8 * (rows // 8 + 1 - rows // 8 % 2)
     step = -(-(rows + 4) // 16) * 16
     dims = (n_lat, n_lon, chans, rows, wide, slots, hid)
     vmem = pl.BlockSpec(memory_space=pltpu.VMEM)
+    hbm = pl.BlockSpec(memory_space=pltpu.HBM)
     features, tile = pl.pallas_call(
         functools.partial(kernel, dims),
         out_shape=(
-            jax.ShapeDtypeStruct((rows * wide, hid), BF16),
+            jax.ShapeDtypeStruct((hid, rows, wide), BF16),
             jax.ShapeDtypeStruct((chans, rows, wide), BF16),
         ),
         in_specs=[
-            vmem, pl.BlockSpec(memory_space=pl.ANY), pl.BlockSpec(memory_space=pltpu.SMEM),
-            vmem, vmem, vmem, vmem,
+            hbm, hbm, hbm, hbm, hbm, hbm, hbm,
         ],
         out_specs=(vmem, vmem),
         scratch_shapes=[
-            pltpu.VMEM((cp * rows, wide), F32),
+            pltpu.VMEM((chans, rows, wide), BF16),
+            pltpu.VMEM((9, chans, hid), BF16),
+            pltpu.VMEM((9, hid, hid), BF16),
+            pltpu.VMEM((1, hid), F32),
+            pltpu.VMEM((1, hid), F32),
+            pltpu.SMEM((chans,), jnp.int32),
+            pltpu.VMEM((hid, pitch, wide), F32),
+            pltpu.SemaphoreType.DMA((6,)),
+            pltpu.VMEM((cp, pitch, wide), F32),
             pltpu.VMEM((rows + 4, wide, kp), BF16),
             pltpu.VMEM((2, 2 * rows, kp), F32),
             pltpu.VMEM((2, 2 * rows + 16, kp), F32),
@@ -291,13 +325,18 @@
             pltpu.SemaphoreType.DMA,
         ],
         compiler_params=pltpu.CompilerParams(
-            collective_id=0, has_side_effects=True, vmem_limit_bytes=60 * 1024 * 1024
+            collective_id=0, has_side_effects=True, vmem_limit_bytes=32 * 1024 * 1024
         ),
     )(
-        current.reshape(chans * rows, wide), next_fields, reader_slot,
-        first_weight.transpose(0, 2, 1), first_bias[None], second_weight, second_bias[None],
+        *[
+            pltpu.with_memory_space_constraint(x, pltpu.HBM)
+            for x in (
+                current, next_fields, reader_slot, first_weight.transpose(0, 2, 1),
+                first_bias[None], second_weight, second_bias[None],
+            )
+        ]
     )
-    return features.reshape(rows, wide, hid).transpose(2, 0, 1), tile
+    return features, tile
 
 
 def solution(mesh):

time: 42.4 us -> 34.1 us (0.80)
  the two profiles are of different devices: /device:TPU:0 before, /device:TPU:9 now
where the time goes in v2:
time: 34.1 us; the launch traced here: 33.9 us
  Pallas kernels  31.1 us (91%)
  local copies, waits for them, and re-layouts  2.13 us (6%)
  between operations  0.64 us (2%)
    pallas_call x1, Pallas kernels, body(): pl.pallas_call(functools.partial(kernel, dims), out_shape=(jax.ShapeDtype...  31.1 us
    unnamed x2, local copies, waits for them, and re-layouts  2.13 us

profile of v2, /device:TPU:9, one launch (start us, length us, event | category | flops | bytes accessed | tf_op | source)
XLA Modules:
  0.0 33.9 jit_solution(7543406882664136832)
XLA Ops:
  0.6 31.1 %shard_map.86 = (bf16[256,32,128]{2,1,0:T(8,128)(2,1)S(1)}, bf16[69,32,128]{2,1,0:T(8,128)(2,1)S(1)}) custom-call(bf16[69,32,128]{2,1,0:T(8,128)(2,1)} %cur_in.1, bf16[3,256,512]{2,1,0:T(8,128)(2,1)} %nf.1, s32[69]{0:T(128)} %slot_in.1, bf16[9,69,256]{2,1,0:T(8,128)(2,1)} %bitcast.3, f32[1,256]{1,0:T(1,128)} %bitcast.4, bf16[9,256,256]{2,1,0:T(8,128)(2,1)} %w2_in.1, ...), custom_call_target="tpu_custom_call" | custom-call | tf_op jit(solution)/shard_map/pallas_call | solution.py:288
  31.8 1.3 %copy.11 = bf16[256,32,128]{2,1,0:T(8,128)(2,1)} copy(bf16[256,32,128]{2,1,0:T(8,128)(2,1)S(1)} %get-tuple-element.4) | data formatting | bytes 4194304
  33.1 0.8 %copy.12 = bf16[69,32,128]{2,1,0:T(8,128)(2,1)} copy(bf16[69,32,128]{2,1,0:T(8,128)(2,1)S(1)} %get-tuple-element.5) | data formatting | bytes 1130496
